TPU v7x, 32 devices: a whole 2x2x4 slice. The times are simulated.
32 devices in a mesh: mp: 8 (over y, x, core), hidden: 4 (over z).
Axes of the slice: x: 2, y: 2, z: 4, core: 2. Of those that a mesh axis runs over, the one named last changes fastest.
Arguments:
- states: bfloat16 [512, 16384], P(None, 'mp'), may hold values from -6 to 6
- gate_codes: bfloat16 [16384, 26624], P('mp', 'hidden'), may hold values from -127 to 127, as said below
- gate_scales: float32 [128, 26624], P('mp', 'hidden'), may hold values from 7.8125e-05 to 0.000703125
- up_codes: bfloat16 [16384, 26624], P('mp', 'hidden'), may hold values from -127 to 127, as said below
- up_scales: float32 [128, 26624], P('mp', 'hidden'), may hold values from 7.8125e-05 to 0.000703125
- down_codes: bfloat16 [26624, 16384], P('hidden', 'mp'), may hold values from -127 to 127, as said below
- down_scales: float32 [208, 16384], P('hidden', 'mp'), may hold values from 1.2257258e-05 to 0.000110315326
Outputs:
- output: bfloat16 [512, 16384], P(None, 'mp')
Inputs may be any that keep to these rules, and one draw needn't show every extreme that they name: `gate_codes`: whole numbers. `up_codes`: whole numbers. `down_codes`: whole numbers.
All inputs are finite; a program needn't handle non-finite values. Where the computation divides by a largest or mean magnitude, that divisor is 1e-20 or more.
Results may differ from a plain program's by a relative error of at most 0.02.
Values may be sent and summed in bfloat16 or wider, within the bound.
A program may use at most 256 MiB of HBM per device.

v0:
```python
import jax
import jax.numpy as jnp
from jax import lax
from jax.sharding import PartitionSpec as P

BLOCK = 128
epsilon = 1e-06


def dequantize(quantized, scales):
    depth, columns = quantized.shape
    groups = scales.shape[0]
    blocks = quantized.astype(jnp.float32).reshape(groups, depth // groups, columns)
    return (blocks * scales[:, None, :]).reshape(depth, columns).astype(jnp.bfloat16)


def encode(values):
    row_count, columns = values.shape
    blocks = values.reshape(row_count, columns // BLOCK, BLOCK)
    maxima = (jnp.max(jnp.abs(blocks), axis=-1) + epsilon).astype(jnp.bfloat16)
    factor = 127.0 / maxima.astype(jnp.float32)
    codes = (blocks * factor[..., None]).astype(jnp.bfloat16)
    return (codes.reshape(row_count, columns), maxima)


def decode(codes, maxima):
    row_count, columns = codes.shape
    blocks = codes.astype(jnp.float32).reshape(row_count, columns // BLOCK, BLOCK)
    step_size = maxima.astype(jnp.float32) / 127.0
    return (blocks * step_size[..., None]).reshape(row_count, columns)


def body(states, gate_codes, gate_scales, up_codes, up_scales, down_codes, down_scales):
    gate_w = dequantize(gate_codes, gate_scales)
    up_w = dequantize(up_codes, up_scales)
    columns = gate_w.shape[1]
    row_count = states.shape[0]
    senders = lax.axis_size("mp")
    own_rows = row_count // senders
    gate_part = jnp.dot(states, gate_w, preferred_element_type=jnp.float32)
    up_part = jnp.dot(states, up_w, preferred_element_type=jnp.float32)
    gate_enc, gate_max = encode(gate_part)
    up_enc, up_max = encode(up_part)
    codes = jnp.concatenate([gate_enc, up_enc], axis=1)
    scales = jnp.concatenate([gate_max, up_max], axis=1)
    got_codes, got_scales = (
        lax.all_to_all(codes, "mp", split_axis=0, concat_axis=0, tiled=True),
        lax.all_to_all(scales, "mp", split_axis=0, concat_axis=0, tiled=True),
    )
    summed = decode(got_codes, got_scales).reshape(senders, own_rows, 2 * columns).sum(axis=0)
    swiglu = jax.nn.silu(summed[:, :columns]) * summed[:, columns:]
    act_codes, act_scales = encode(swiglu)
    all_codes, all_scales = (
        lax.all_gather(act_codes, "mp", axis=0, tiled=True),
        lax.all_gather(act_scales, "mp", axis=0, tiled=True),
    )
    activation = decode(all_codes, all_scales).astype(jnp.bfloat16)
    down_w = dequantize(down_codes, down_scales)
    whole_sum = lax.psum(
        jnp.dot(activation, down_w, preferred_element_type=jnp.float32).astype(jnp.bfloat16),
        "hidden",
    ).astype(jnp.float32)
    return (whole_sum + states.astype(jnp.float32)).astype(jnp.bfloat16)


def solution(mesh):
    in_specs = (
        P(None, "mp"),
        P("mp", "hidden"),
        P("mp", "hidden"),
        P("mp", "hidden"),
        P("mp", "hidden"),
        P("hidden", "mp"),
        P("hidden", "mp"),
    )
    out_specs = P(None, "mp")
    return jax.shard_map(body, mesh=mesh, in_specs=in_specs, out_specs=out_specs, check_vma=False)
```

profile of v0, /device:TPU:0, one launch (start us, length us, event | category | flops | bytes accessed | tf_op | source)
XLA Modules:
  0.0 518.5 jit_solution(13430339111039711883)
XLA Ops:
  6.5 19.5 %fusion.2 = bf16[2048,6656]{1,0:T(8,128)(2,1)} fusion(bf16[2048,6656]{1,0:T(8,128)(2,1)} %param.8, f32[16,6656]{1,0:T(8,128)} %param.9), kind=kLoop, calls=%fused_computation.5 | loop fusion | flops 40894464 | bytes 54951936 | tf_op jit(solution)/shard_map/convert_element_type | solution.py:14
  26.0 25.2 %bitcast_abs_fusion.1 = (f32[512,6656]{0,1:T(8,128)}, f32[6656,512]{1,0:T(8,128)}) fusion(bf16[2048,6656]{1,0:T(8,128)(2,1)} %fusion.2, bf16[512,2048]{1,0:T(8,128)(2,1)S(1)} %copy-done), kind=kOutput, calls=%fused_computation.13 | convolution fusion | flops 13962051584 | bytes 56623104 | tf_op jit(solution)/shard_map/dot_general | solution.py:40
  51.3 7.1 %reduce_max.27 = f32[512,52]{0,1:T(8,128)S(1)} reduce(f32[512,52,128]{0,2,1:T(8,128)} %bitcast.51, f32[]{:T(128)} %constant.7.clone.1), dimensions={2}, to_apply=%region_0.0 | reduce | flops 3381248 | bytes 13737988 | tf_op jit(solution)/shard_map/reduce_max | solution.py:20
  58.5 19.0 %fusion.1 = bf16[2048,6656]{1,0:T(8,128)(2,1)} fusion(bf16[2048,6656]{1,0:T(8,128)(2,1)} %param.10, f32[16,6656]{1,0:T(8,128)S(1)} %copy-done.2), kind=kLoop, calls=%fused_computation.3 | loop fusion | flops 40894464 | bytes 54951936 | tf_op jit(solution)/shard_map/convert_element_type | solution.py:14
  77.6 25.5 %bitcast_abs_fusion = (f32[512,6656]{0,1:T(8,128)}, f32[6656,512]{1,0:T(8,128)}) fusion(bf16[2048,6656]{1,0:T(8,128)(2,1)} %fusion.1, bf16[512,2048]{1,0:T(8,128)(2,1)S(1)} %copy-done), kind=kOutput, calls=%fused_computation.10 | convolution fusion | flops 13962051584 | bytes 56623104 | tf_op jit(solution)/shard_map/dot_general | solution.py:41
  103.1 7.0 %reduce_max.28 = f32[512,52]{0,1:T(8,128)S(1)} reduce(f32[512,52,128]{0,2,1:T(8,128)} %bitcast.52, f32[]{:T(128)} %constant.7.clone.1), dimensions={2}, to_apply=%region_1.0 | reduce | flops 3381248 | bytes 13737988 | tf_op jit(solution)/shard_map/reduce_max | solution.py:20
  111.0 5.2 %all-to-all-start.1 = ((bf16[8,64,104]{2,1,0:T(8,128)(2,1)}), bf16[8,64,104]{2,1,0:T(8,128)(2,1)S(1)}, u32[]{:S(2)}, u32[]{:S(2)}) async-start(bf16[8,64,104]{2,1,0:T(8,128)(2,1)} %pad_maximum_fusion.1), calls=%async_computation.1 | async-start | bytes 262144 | tf_op jit(solution)/shard_map/all_to_all | solution.py:48
  116.2 9.7 %fusion.4 = bf16[512,6656]{0,1:T(8,128)(2,1)} fusion(f32[6656,512]{1,0:T(8,128)} %get-tuple-element.14, f32[512,52]{0,1:T(8,128)S(1)} %get-tuple-element.5), kind=kLoop, calls=%fused_computation.12 | loop fusion | flops 6815744 | bytes 20553728 | tf_op jit(solution)/shard_map/convert_element_type | solution.py:22
  125.9 10.0 %copy.34 = bf16[512,6656]{1,0:T(8,128)(2,1)} copy(bf16[512,6656]{0,1:T(8,128)(2,1)} %fusion.4) | data formatting | bytes 13631488 | tf_op jit(solution)/shard_map/convert_element_type | solution.py:22
  135.9 9.6 %fusion.3 = bf16[512,6656]{0,1:T(8,128)(2,1)} fusion(f32[6656,512]{1,0:T(8,128)} %get-tuple-element.12, f32[512,52]{0,1:T(8,128)S(1)} %get-tuple-element.7), kind=kLoop, calls=%fused_computation.9 | loop fusion | flops 6815744 | bytes 20553728 | tf_op jit(solution)/shard_map/convert_element_type | solution.py:22
  145.5 9.8 %copy.35 = bf16[512,6656]{1,0:T(8,128)(2,1)} copy(bf16[512,6656]{0,1:T(8,128)(2,1)} %fusion.3) | data formatting | bytes 13631488 | tf_op jit(solution)/shard_map/convert_element_type | solution.py:22
  155.3 11.8 %pad_maximum_fusion = bf16[8,64,13312]{2,1,0:T(8,128)(2,1)} fusion(bf16[8,64,6656]{2,1,0:T(8,128)(2,1)} %bitcast.50, bf16[8,64,6656]{2,1,0:T(8,128)(2,1)} %bitcast.49), kind=kLoop, calls=%fused_computation.7 | loop fusion | flops 27262976 | bytes 27262976 | tf_op jit(solution)/shard_map/concatenate | solution.py:44
  167.1 5.5 %all-to-all-start = ((bf16[8,64,13312]{2,1,0:T(8,128)(2,1)}), bf16[8,64,13312]{2,1,0:T(8,128)(2,1)}, u32[]{:S(2)}, u32[]{:S(2)}) async-start(bf16[8,64,13312]{2,1,0:T(8,128)(2,1)} %pad_maximum_fusion), calls=%async_computation | async-start | bytes 27262976 | tf_op jit(solution)/shard_map/all_to_all | solution.py:47
  172.7 9.5 %mul.107 = f32[512,104,128]{2,1,0:T(8,128)} broadcast(f32[512,104]{1,0:T(8,128)S(1)} %bitcast.54), dimensions={0,1} | broadcast | bytes 27475968 | tf_op jit(solution)/shard_map/mul | solution.py:30
  182.2 27.5 %mul.108 = f32[8,64,13312]{2,1,0:T(8,128)} reshape(f32[512,104,128]{2,1,0:T(8,128)} %mul.107) | data formatting | bytes 54525952 | tf_op jit(solution)/shard_map/mul | solution.py:30
  209.7 113.1 %all-to-all-done = bf16[8,64,13312]{2,1,0:T(8,128)(2,1)} async-done(((bf16[8,64,13312]{2,1,0:T(8,128)(2,1)}), bf16[8,64,13312]{2,1,0:T(8,128)(2,1)}, u32[]{:S(2)}, u32[]{:S(2)}) %all-to-all-start) | async-done | bytes 13631520 | tf_op jit(solution)/shard_map/all_to_all | solution.py:47
  322.8 14.5 %multiply_reduce_fusion = f32[64,13312]{1,0:T(8,128)S(1)} fusion(f32[8,64,13312]{2,1,0:T(8,128)} %mul.108, bf16[8,64,13312]{2,1,0:T(8,128)(2,1)} %all-to-all-done), kind=kLoop, calls=%fused_computation.6 | loop fusion | flops 19595264 | bytes 44302336 | tf_op jit(solution)/shard_map/reduce_sum | solution.py:50
  345.8 19.6 %fusion = bf16[6656,2048]{1,0:T(8,128)(2,1)} fusion(bf16[6656,2048]{1,0:T(8,128)(2,1)} %param.12, f32[52,2048]{1,0:T(8,128)} %param.13), kind=kLoop, calls=%fused_computation.1 | loop fusion | flops 40894464 | bytes 54951936 | tf_op jit(solution)/shard_map/convert_element_type | solution.py:14
  365.5 8.5 %all-gather = bf16[8,64,52]{1,2,0:T(8,128)(2,1)S(1)} all-gather(bf16[1,64,52]{1,2,0:T(8,128)(2,1)S(1)} %copy.38), channel_id=1, replica_groups=mesh['mp'=8,'hidden'=4] {'mp'}, dimensions={0}, use_global_device_ids=true | all-gather | bytes 59904 | tf_op jit(solution)/shard_map/all_gather | solution.py:55
  374.1 6.6 %mul.115 = f32[512,52,128]{0,2,1:T(8,128)} broadcast(f32[512,52]{0,1:T(8,128)S(1)} %reshape.78), dimensions={0,1} | broadcast | bytes 13737984 | tf_op jit(solution)/shard_map/mul | solution.py:30
  380.7 14.6 %copy.40 = f32[512,6656]{1,0:T(8,128)} copy(f32[512,6656]{0,1:T(8,128)} %bitcast.48) | data formatting | bytes 27262976 | tf_op jit(solution)/shard_map/mul | solution.py:30
  395.3 26.2 %fusion.6 = bf16[512,2048]{1,0:T(8,128)(2,1)} fusion(bf16[6656,2048]{1,0:T(8,128)(2,1)} %fusion, f32[512,6656]{1,0:T(8,128)} %copy.40, bf16[512,6656]{1,0:T(8,128)(2,1)} %all-gather.3.cloned.1.call-done), kind=kOutput, calls=%fused_computation.17 | convolution fusion | flops 13969915904 | bytes 49807360 | tf_op jit(solution)/shard_map/dot_general | solution.py:60
  421.5 86.4 %all-reduce.2.cloned.1.call-done = bf16[512,2048]{1,0:T(8,128)(2,1)} async-done(((bf16[512,2048]{1,0:T(8,128)(2,1)}), bf16[512,2048]{1,0:T(8,128)(2,1)}) %all-reduce.2.cloned.1.call-update) | async-done | bytes 2097168 | tf_op jit(solution)/shard_map/psum | solution.py:59
  508.0 3.7 add_convert_fusion
  (27 shorter events, 9.8 us)
Async XLA Ops:
  6.5 19.5 %copy-start = (bf16[512,2048]{1,0:T(8,128)(2,1)S(1)}, bf16[512,2048]{1,0:T(8,128)(2,1)}, u32[]{:S(2)}) copy-start(bf16[512,2048]{1,0:T(8,128)(2,1)} %param.7) | copy-start | bytes 6291460
  51.3 7.3 %copy-start.2 = (f32[16,6656]{1,0:T(8,128)S(1)}, f32[16,6656]{1,0:T(8,128)}, u32[]{:S(2)}) copy-start(f32[16,6656]{1,0:T(8,128)} %param.11) | copy-start | bytes 1277956
  111.0 56.1 %all-to-all-start.1 = ((bf16[8,64,104]{2,1,0:T(8,128)(2,1)}), bf16[8,64,104]{2,1,0:T(8,128)(2,1)S(1)}, u32[]{:S(2)}, u32[]{:S(2)}) async-start(bf16[8,64,104]{2,1,0:T(8,128)(2,1)} %pad_maximum_fusion.1), calls=%async_computation.1 | async-start | bytes 262144 | tf_op jit(solution)/shard_map/all_to_all | solution.py:48
  167.1 155.7 %all-to-all-start = ((bf16[8,64,13312]{2,1,0:T(8,128)(2,1)}), bf16[8,64,13312]{2,1,0:T(8,128)(2,1)}, u32[]{:S(2)}, u32[]{:S(2)}) async-start(bf16[8,64,13312]{2,1,0:T(8,128)(2,1)} %pad_maximum_fusion), calls=%async_computation | async-start | bytes 27262976 | tf_op jit(solution)/shard_map/all_to_all | solution.py:47
  172.6 222.7 %all-gather.3.cloned.1.call-start = ((), (), s32[]{:S(2)}) async-start(), calls=%async_computation.2 | async-start | bytes 7667712 | tf_op jit(solution)/shard_map/all_gather | solution.py:54
  345.7 162.2 %all-reduce.2.cloned.1.call-start = ((), (), s32[]{:S(2)}) async-start(), calls=%async_computation.3 | async-start | bytes 4194304 | tf_op jit(solution)/shard_map/psum | solution.py:59
  395.3 112.7 %copy-start.1 = (bf16[512,2048]{1,0:T(8,128)(2,1)S(1)}, bf16[512,2048]{1,0:T(8,128)(2,1)}, u32[]{:S(2)}) copy-start(bf16[512,2048]{1,0:T(8,128)(2,1)} %param.7) | copy-start | bytes 6291460
Sparse Core Ops, SparseCore 0:
  345.9 47.1 all-gather.2
  421.7 86.2 all-reduce.1
where the time goes:
time: 521 us; the launch traced here: 519 us
  waiting for transfers between devices  200 us (38%)
  other arithmetic  128 us (25%)
  local copies, waits for them, and re-layouts  81.6 us (16%)
  matrix products  76.9 us (15%)
  between operations  13.5 us (3%)
  starting transfers between devices  10.8 us (2%)
  blocking collectives  8.49 us (2%)
    all_to_all x1, waiting for transfers between devices, body(): lax.all_to_all(codes, 'mp', split_axis=0, concat_axis=0, tiled=True)  113 us
    psum x1, waiting for transfers between devices, body(): lax.psum(jnp.dot(activation, down_w, preferred_element_type=jnp.float32)....  86.4 us
    mul x4, local copies, waits for them, and re-layouts, decode(): return (blocks * step_size[..., None]).reshape(row_count, columns)  58.2 us
    convert_element_type x3, other arithmetic, dequantize(): (blocks * scales[:, None, :]).reshape(depth, columns).astype(jnp.bfloat16)  58.1 us
    dot_general x1, matrix products, body(): jnp.dot(activation, down_w, preferred_element_type=jnp.float32)  26.2 us
    dot_general x1, matrix products, body(): up_part = jnp.dot(states, up_w, preferred_element_type=jnp.float32)  25.5 us
    dot_general x1, matrix products, body(): gate_part = jnp.dot(states, gate_w, preferred_element_type=jnp.float32)  25.2 us
    convert_element_type x3, other arithmetic, encode(): codes = (blocks * factor[..., None]).astype(jnp.bfloat16)  20.8 us
  transfers between devices with their start and end apart: 4, of which 2 were waited for; matrix products, arithmetic and copies ran while one was open for 25% of the time, Pallas kernels for 0%

commit v1 on v0

--- a/solution.py
+++ b/solution.py
@@ -56,9 +56,12 @@
     )
     activation = decode(all_codes, all_scales).astype(jnp.bfloat16)
     down_w = dequantize(down_codes, down_scales)
-    whole_sum = lax.psum(
-        jnp.dot(activation, down_w, preferred_element_type=jnp.float32).astype(jnp.bfloat16),
-        "hidden",
+    whole_sum = jnp.sum(
+        lax.all_gather(
+            jnp.dot(activation, down_w, preferred_element_type=jnp.float32).astype(jnp.bfloat16),
+            "hidden",
+        ),
+        axis=0,
     ).astype(jnp.float32)
     return (whole_sum + states.astype(jnp.float32)).astype(jnp.bfloat16)
 

time: 521 us -> 597 us (1.15)
  waiting for transfers between devices: 200 us -> 263 us
    all_gather x0 -> x1, waiting for transfers between devices: none -> 150 us  [body(): lax.all_gather(jnp.dot(activation, down_w, preferred_element_type=jnp.flo...]
    psum x1 -> x0, waiting for transfers between devices: 86.4 us -> none  [body(): lax.psum(jnp.dot(activation, down_w, preferred_element_type=jnp.float32)....]
  transfers between devices with their start and end apart: 4 -> 4, of which waited for: 2 -> 2; matrix products, arithmetic and copies ran while one was open for 25% -> 22% of each run, Pallas kernels for 0% -> 0%
where the time goes in v1:
time: 597 us; the launch traced here: 589 us
  waiting for transfers between devices  263 us (44%)
  other arithmetic  133 us (22%)
  local copies, waits for them, and re-layouts  81.9 us (14%)
  matrix products  77.2 us (13%)
  between operations  13.7 us (2%)
  starting transfers between devices  11 us (2%)
  blocking collectives  8.5 us (1%)
    all_gather x1, waiting for transfers between devices, body(): lax.all_gather(jnp.dot(activation, down_w, preferred_element_type=jnp.flo...  150 us
    all_to_all x1, waiting for transfers between devices, body(): lax.all_to_all(codes, 'mp', split_axis=0, concat_axis=0, tiled=True)  113 us
    mul x4, local copies, waits for them, and re-layouts, decode(): return (blocks * step_size[..., None]).reshape(row_count, columns)  58.3 us
    convert_element_type x3, other arithmetic, dequantize(): (blocks * scales[:, None, :]).reshape(depth, columns).astype(jnp.bfloat16)  58.2 us
    dot_general x1, matrix products, body(): jnp.dot(activation, down_w, preferred_element_type=jnp.float32)  26.3 us
    dot_general x1, matrix products, body(): up_part = jnp.dot(states, up_w, preferred_element_type=jnp.float32)  25.7 us
    dot_general x1, matrix products, body(): gate_part = jnp.dot(states, gate_w, preferred_element_type=jnp.float32)  25.2 us
    convert_element_type x3, other arithmetic, encode(): codes = (blocks * factor[..., None]).astype(jnp.bfloat16)  20.8 us
  transfers between devices with their start and end apart: 4, of which 2 were waited for; matrix products, arithmetic and copies ran while one was open for 22% of the time, Pallas kernels for 0%

profile of v1, /device:TPU:0, one launch (start us, length us, event | category | flops | bytes accessed | tf_op | source)
XLA Modules:
  0.0 588.8 jit_solution(9852118269134284058)
XLA Ops:
  6.5 19.5 %fusion.2 = bf16[2048,6656]{1,0:T(8,128)(2,1)} fusion(bf16[2048,6656]{1,0:T(8,128)(2,1)} %param.8, f32[16,6656]{1,0:T(8,128)} %param.9), kind=kLoop, calls=%fused_computation.5 | loop fusion | flops 40894464 | bytes 54951936 | tf_op jit(solution)/shard_map/convert_element_type | solution.py:14
  26.1 25.2 %bitcast_abs_fusion.1 = (f32[512,6656]{0,1:T(8,128)}, f32[6656,512]{1,0:T(8,128)}) fusion(bf16[2048,6656]{1,0:T(8,128)(2,1)} %fusion.2, bf16[512,2048]{1,0:T(8,128)(2,1)S(1)} %copy-done), kind=kOutput, calls=%fused_computation.13 | convolution fusion | flops 13962051584 | bytes 56623104 | tf_op jit(solution)/shard_map/dot_general | solution.py:40
  51.3 7.1 %reduce_max.27 = f32[512,52]{0,1:T(8,128)S(1)} reduce(f32[512,52,128]{0,2,1:T(8,128)} %bitcast.52, f32[]{:T(128)} %constant.4.clone.1), dimensions={2}, to_apply=%region_0.0 | reduce | flops 3381248 | bytes 13737988 | tf_op jit(solution)/shard_map/reduce_max | solution.py:20
  58.5 19.1 %fusion.1 = bf16[2048,6656]{1,0:T(8,128)(2,1)} fusion(bf16[2048,6656]{1,0:T(8,128)(2,1)} %param.10, f32[16,6656]{1,0:T(8,128)S(1)} %copy-done.1), kind=kLoop, calls=%fused_computation.3 | loop fusion | flops 40894464 | bytes 54951936 | tf_op jit(solution)/shard_map/convert_element_type | solution.py:14
  77.6 25.7 %bitcast_abs_fusion = (f32[512,6656]{0,1:T(8,128)}, f32[6656,512]{1,0:T(8,128)}) fusion(bf16[2048,6656]{1,0:T(8,128)(2,1)} %fusion.1, bf16[512,2048]{1,0:T(8,128)(2,1)S(1)} %copy-done), kind=kOutput, calls=%fused_computation.10 | convolution fusion | flops 13962051584 | bytes 56623104 | tf_op jit(solution)/shard_map/dot_general | solution.py:41
  103.4 7.0 %reduce_max.28 = f32[512,52]{0,1:T(8,128)S(1)} reduce(f32[512,52,128]{0,2,1:T(8,128)} %bitcast.53, f32[]{:T(128)} %constant.4.clone.1), dimensions={2}, to_apply=%region_1.0 | reduce | flops 3381248 | bytes 13737988 | tf_op jit(solution)/shard_map/reduce_max | solution.py:20
  111.3 5.4 all-to-all-start.1
  116.8 9.7 %fusion.4 = bf16[512,6656]{0,1:T(8,128)(2,1)} fusion(f32[6656,512]{1,0:T(8,128)} %get-tuple-element.14, f32[512,52]{0,1:T(8,128)S(1)} %get-tuple-element.5), kind=kLoop, calls=%fused_computation.12 | loop fusion | flops 6815744 | bytes 20553728 | tf_op jit(solution)/shard_map/convert_element_type | solution.py:22
  126.5 10.0 %copy.34 = bf16[512,6656]{1,0:T(8,128)(2,1)} copy(bf16[512,6656]{0,1:T(8,128)(2,1)} %fusion.4) | data formatting | bytes 13631488 | tf_op jit(solution)/shard_map/convert_element_type | solution.py:22
  136.4 9.6 %fusion.3 = bf16[512,6656]{0,1:T(8,128)(2,1)} fusion(f32[6656,512]{1,0:T(8,128)} %get-tuple-element.12, f32[512,52]{0,1:T(8,128)S(1)} %get-tuple-element.7), kind=kLoop, calls=%fused_computation.9 | loop fusion | flops 6815744 | bytes 20553728 | tf_op jit(solution)/shard_map/convert_element_type | solution.py:22
  146.0 10.0 %copy.35 = bf16[512,6656]{1,0:T(8,128)(2,1)} copy(bf16[512,6656]{0,1:T(8,128)(2,1)} %fusion.3) | data formatting | bytes 13631488 | tf_op jit(solution)/shard_map/convert_element_type | solution.py:22
  156.0 11.8 %pad_maximum_fusion = bf16[8,64,13312]{2,1,0:T(8,128)(2,1)} fusion(bf16[8,64,6656]{2,1,0:T(8,128)(2,1)} %bitcast.51, bf16[8,64,6656]{2,1,0:T(8,128)(2,1)} %bitcast.50), kind=kLoop, calls=%fused_computation.7 | loop fusion | flops 27262976 | bytes 27262976 | tf_op jit(solution)/shard_map/concatenate | solution.py:44
  167.8 5.5 all-to-all-start
  173.4 9.5 %mul.107 = f32[512,104,128]{2,1,0:T(8,128)} broadcast(f32[512,104]{1,0:T(8,128)S(1)} %bitcast.56), dimensions={0,1} | broadcast | bytes 27475968 | tf_op jit(solution)/shard_map/mul | solution.py:30
  182.9 27.5 %mul.108 = f32[8,64,13312]{2,1,0:T(8,128)} reshape(f32[512,104,128]{2,1,0:T(8,128)} %mul.107) | data formatting | bytes 54525952 | tf_op jit(solution)/shard_map/mul | solution.py:30
  210.4 113.1 %all-to-all-done = bf16[8,64,13312]{2,1,0:T(8,128)(2,1)} async-done(((bf16[8,64,13312]{2,1,0:T(8,128)(2,1)}), bf16[8,64,13312]{2,1,0:T(8,128)(2,1)}, u32[]{:S(2)}, u32[]{:S(2)}) %all-to-all-start) | async-done | bytes 13631520 | tf_op jit(solution)/shard_map/all_to_all | solution.py:47
  323.5 14.5 %multiply_reduce_fusion = f32[64,13312]{1,0:T(8,128)S(1)} fusion(f32[8,64,13312]{2,1,0:T(8,128)} %mul.108, bf16[8,64,13312]{2,1,0:T(8,128)(2,1)} %all-to-all-done), kind=kLoop, calls=%fused_computation.6 | loop fusion | flops 19595264 | bytes 44302336 | tf_op jit(solution)/shard_map/reduce_sum | solution.py:50
  346.5 19.6 %fusion = bf16[6656,2048]{1,0:T(8,128)(2,1)} fusion(bf16[6656,2048]{1,0:T(8,128)(2,1)} %param.12, f32[52,2048]{1,0:T(8,128)} %param.13), kind=kLoop, calls=%fused_computation.1 | loop fusion | flops 40894464 | bytes 54951936 | tf_op jit(solution)/shard_map/convert_element_type | solution.py:14
  366.2 8.5 %all-gather.1 = bf16[8,64,52]{1,2,0:T(8,128)(2,1)S(1)} all-gather(bf16[1,64,52]{1,2,0:T(8,128)(2,1)S(1)} %copy.38), channel_id=1, replica_groups=mesh['mp'=8,'hidden'=4] {'mp'}, dimensions={0}, use_global_device_ids=true | all-gather | bytes 59904 | tf_op jit(solution)/shard_map/all_gather | solution.py:55
  374.8 6.6 %mul.115 = f32[512,52,128]{0,2,1:T(8,128)} broadcast(f32[512,52]{0,1:T(8,128)S(1)} %reshape.79), dimensions={0,1} | broadcast | bytes 13737984 | tf_op jit(solution)/shard_map/mul | solution.py:30
  381.4 14.7 %copy.40 = f32[512,6656]{1,0:T(8,128)} copy(f32[512,6656]{0,1:T(8,128)} %bitcast.49) | data formatting | bytes 27262976 | tf_op jit(solution)/shard_map/mul | solution.py:30
  396.1 26.3 %fusion.6 = bf16[512,2048]{1,0:T(8,128)(2,1)} fusion(bf16[6656,2048]{1,0:T(8,128)(2,1)} %fusion, f32[512,6656]{1,0:T(8,128)} %copy.40, bf16[512,6656]{1,0:T(8,128)(2,1)} %all-gather.5.cloned.1.call-done), kind=kOutput, calls=%fused_computation.17 | convolution fusion | flops 13969915904 | bytes 49807360 | tf_op jit(solution)/shard_map/dot_general | solution.py:61
  422.3 150.0 %all-gather.7.cloned.1.call-done = bf16[2048,2048]{1,0:T(8,128)(2,1)} async-done(((bf16[512,2048]{1,0:T(8,128)(2,1)}), bf16[2048,2048]{1,0:T(8,128)(2,1)}) %all-gather.7.cloned.1.call-update) | async-done | bytes 8388624 | tf_op jit(solution)/shard_map/all_gather | solution.py:60
  572.3 5.7 reduce_sum.22
  (26 shorter events, 13.5 us)
Async XLA Ops:
  6.5 19.5 %copy-start = (bf16[512,2048]{1,0:T(8,128)(2,1)S(1)}, bf16[512,2048]{1,0:T(8,128)(2,1)}, u32[]{:S(2)}) copy-start(bf16[512,2048]{1,0:T(8,128)(2,1)} %param.7) | copy-start | bytes 6291460
  51.3 7.3 %copy-start.1 = (f32[16,6656]{1,0:T(8,128)S(1)}, f32[16,6656]{1,0:T(8,128)}, u32[]{:S(2)}) copy-start(f32[16,6656]{1,0:T(8,128)} %param.11) | copy-start | bytes 1277956
  111.3 56.5 %all-to-all-start.1 = ((bf16[8,64,104]{2,1,0:T(8,128)(2,1)}), bf16[8,64,104]{2,1,0:T(8,128)(2,1)S(1)}, u32[]{:S(2)}, u32[]{:S(2)}) async-start(bf16[8,64,104]{2,1,0:T(8,128)(2,1)} %pad_maximum_fusion.1), calls=%async_computation.1 | async-start | bytes 262144 | tf_op jit(solution)/shard_map/all_to_all | solution.py:48
  167.8 155.7 %all-to-all-start = ((bf16[8,64,13312]{2,1,0:T(8,128)(2,1)}), bf16[8,64,13312]{2,1,0:T(8,128)(2,1)}, u32[]{:S(2)}, u32[]{:S(2)}) async-start(bf16[8,64,13312]{2,1,0:T(8,128)(2,1)} %pad_maximum_fusion), calls=%async_computation | async-start | bytes 27262976 | tf_op jit(solution)/shard_map/all_to_all | solution.py:47
  173.3 222.8 %all-gather.5.cloned.1.call-start = ((), (), s32[]{:S(2)}) async-start(), calls=%async_computation.2 | async-start | bytes 7667712 | tf_op jit(solution)/shard_map/all_gather | solution.py:54
  346.4 225.9 %all-gather.7.cloned.1.call-start = ((), (), s32[]{:S(2)}) async-start(), calls=%async_computation.3 | async-start | bytes 10485760 | tf_op jit(solution)/shard_map/all_gather | solution.py:60
Sparse Core Ops, SparseCore 0:
  346.5 47.1 all-gather.4
  422.5 149.7 all-gather.6
